TPU v7x, 128 devices: a whole 4x4x4 slice. The times are simulated.
128 devices in a mesh: rows: 16 (over z, y), cols: 8 (over x, core).
Axes of the slice: x: 4, y: 4, z: 4, core: 2. Of those that a mesh axis runs over, the one named last changes fastest.
Arguments:
- grad_stack: float32 [512, 64, 2048], P(None, 'rows', 'cols'), may hold values from -6 to 6
- moment_stack: float32 [512, 64, 2048], P(None, 'rows', 'cols'), may hold values from -6 to 6
- weight_stack: float32 [512, 64, 2048], P(None, 'rows', 'cols'), may hold values from -0.1875 to 0.1875
Outputs:
- new_weights: float32 [512, 64, 2048], P(None, 'rows', 'cols')
- new_momentum: float32 [512, 64, 2048], P(None, 'rows', 'cols')
All inputs are finite; a program needn't handle non-finite values.
Results may differ from a plain program's by a relative error of at most 0.0003.
Values sent between devices are 32-bit elements.
A program may use at most 128 MiB of HBM per device.

v0:
```python
import jax
import jax.numpy as jnp
from jax import lax
from jax.sharding import PartitionSpec as P

ITERS = 5


hold_rate = 0.95
learn_rate = 1.0


def on_device(grad_stack, moment_stack, weight_stack):
    new_momentum = hold_rate * moment_stack + grad_stack
    moved = lax.all_to_all(new_momentum, "rows", split_axis=0, concat_axis=1, tiled=True)
    whole = lax.all_to_all(moved, "cols", split_axis=0, concat_axis=2, tiled=True)
    iterate = whole * lax.rsqrt(jnp.sum(whole * whole, axis=(1, 2), keepdims=True) + 1e-06)
    for step in range(ITERS):
        gram = jnp.einsum("mik,mjk->mij", iterate, iterate, precision=lax.Precision.HIGHEST)
        mixed = -4.775 * gram + 2.0315 * jnp.einsum(
            "mij,mjk->mik", gram, gram, precision=lax.Precision.HIGHEST
        )
        iterate = 3.4445 * iterate + jnp.einsum(
            "mij,mjk->mik", mixed, iterate, precision=lax.Precision.HIGHEST
        )
    iterate = lax.all_to_all(iterate, "cols", split_axis=2, concat_axis=0, tiled=True)
    back = lax.all_to_all(iterate, "rows", split_axis=1, concat_axis=0, tiled=True)
    new_weights = weight_stack - learn_rate * back
    return (new_weights, new_momentum)


def solution(mesh):
    placed = (P(None, "rows", "cols"), P(None, "rows", "cols"), P(None, "rows", "cols"))
    return jax.shard_map(
        on_device,
        mesh=mesh,
        in_specs=placed,
        out_specs=(P(None, "rows", "cols"), P(None, "rows", "cols")),
        check_vma=False,
    )
```

profile of v0, /device:TPU:0, one launch (start us, length us, event | category | flops | bytes accessed | tf_op | source)
XLA Modules:
  0.0 191.8 jit_solution(6366112335014375146)
XLA Ops:
  0.6 2.9 %multiply_add_fusion = f32[512,4,256]{2,1,0:T(4,128)S(1)} fusion(f32[512,4,256]{2,1,0:T(4,128)} %param.3, f32[512,4,256]{2,1,0:T(4,128)} %param.4), kind=kLoop, calls=%fused_computation.7 | loop fusion | flops 1048576 | bytes 6291456 | tf_op jit(solution)/shard_map/add | solution.py:14
  3.6 0.0 copy-start
  3.6 37.0 %all_to_all.72 = f32[512,4,256]{2,1,0:T(4,128)S(1)} all-to-all(f32[512,4,256]{2,1,0:T(4,128)S(1)} %multiply_add_fusion), channel_id=1, replica_groups=mesh['rows'=16,'cols'=8] {'rows'}, dimensions={0} | all-to-all | bytes 4194304 | tf_op jit(solution)/shard_map/all_to_all | solution.py:15
  40.6 0.0 copy-done
  40.6 0.4 copy.29
  41.0 0.2 copy.30
  41.2 1.2 copy.31
  42.4 31.4 %all_to_all.73 = f32[32,64,256]{2,1,0:T(8,128)S(1)} all-to-all(f32[32,64,256]{2,1,0:T(8,128)S(1)} %copy.31), channel_id=1, replica_groups=mesh['rows'=16,'cols'=8] {'cols'}, dimensions={0} | all-to-all | bytes 4194304 | tf_op jit(solution)/shard_map/all_to_all | solution.py:16
  73.8 0.3 copy.42
  74.1 0.3 multiply_reduce_fusion
  74.4 2.3 %fusion = f32[4,64,64]{2,1,0:T(8,128)S(1)} fusion(f32[4,64,2048]{2,1,0:T(8,128)S(1)} %bitcast.48, f32[4]{0:T(128)S(1)} %add_rsqrt_fusion), kind=kOutput, calls=%fused_computation.8 | convolution fusion | flops 403177472 | bytes 2162704 | tf_op jit(solution)/shard_map/mik,mjk->mij/dot_general | solution.py:19
  76.7 0.3 fusion.7
  77.0 2.1 %convolution_add_fusion.4 = f32[4,64,2048]{2,1,0:T(8,128)S(1)} fusion(f32[4,64,64]{2,1,0:T(8,128)S(1)} %fusion.7, f32[4,64,2048]{2,1,0:T(8,128)S(1)} %bitcast.49, f32[4]{0:T(128)S(1)} %add_rsqrt_fusion), kind=kOutput, calls=%fused_computation.4 | convolution fusion | flops 404750336 | bytes 4259856 | tf_op jit(solution)/shard_map/mij,mjk->mik/dot_general | solution.py:23
  79.1 2.1 %fusion.10 = f32[4,64,64]{2,1,0:T(8,128)S(1)} fusion(f32[4,64,2048]{2,1,0:T(8,128)S(1)} %convolution_add_fusion.4), kind=kOutput, calls=%fused_computation.24 | convolution fusion | flops 402653184 | bytes 2162688 | tf_op jit(solution)/shard_map/mik,mjk->mij/dot_general | solution.py:19
  81.1 0.3 fusion.6
  81.4 2.1 %convolution_add_fusion.3 = f32[4,64,2048]{2,1,0:T(8,128)S(1)} fusion(f32[4,64,64]{2,1,0:T(8,128)S(1)} %fusion.6, f32[4,64,2048]{2,1,0:T(8,128)S(1)} %convolution_add_fusion.4), kind=kOutput, calls=%fused_computation.3 | convolution fusion | flops 403701760 | bytes 4259840 | tf_op jit(solution)/shard_map/mij,mjk->mik/dot_general | solution.py:23
  83.5 2.1 %fusion.11 = f32[4,64,64]{2,1,0:T(8,128)S(1)} fusion(f32[4,64,2048]{2,1,0:T(8,128)S(1)} %convolution_add_fusion.3), kind=kOutput, calls=%fused_computation.25 | convolution fusion | flops 402653184 | bytes 2162688 | tf_op jit(solution)/shard_map/mik,mjk->mij/dot_general | solution.py:19
  85.6 0.3 fusion.5
  85.9 2.3 %convolution_add_fusion.2 = f32[4,64,2048]{2,1,0:T(8,128)S(1)} fusion(f32[4,64,64]{2,1,0:T(8,128)S(1)} %fusion.5, f32[4,64,2048]{2,1,0:T(8,128)S(1)} %convolution_add_fusion.3), kind=kOutput, calls=%fused_computation.2 | convolution fusion | flops 403701760 | bytes 4259840 | tf_op jit(solution)/shard_map/mij,mjk->mik/dot_general | solution.py:23
  88.2 2.1 %fusion.12 = f32[4,64,64]{2,1,0:T(8,128)S(1)} fusion(f32[4,64,2048]{2,1,0:T(8,128)S(1)} %convolution_add_fusion.2), kind=kOutput, calls=%fused_computation.26 | convolution fusion | flops 402653184 | bytes 2162688 | tf_op jit(solution)/shard_map/mik,mjk->mij/dot_general | solution.py:19
  90.3 0.3 fusion.4
  90.6 2.1 %convolution_add_fusion.1 = f32[4,64,2048]{2,1,0:T(8,128)S(1)} fusion(f32[4,64,64]{2,1,0:T(8,128)S(1)} %fusion.4, f32[4,64,2048]{2,1,0:T(8,128)S(1)} %convolution_add_fusion.2), kind=kOutput, calls=%fused_computation.1 | convolution fusion | flops 403701760 | bytes 4259840 | tf_op jit(solution)/shard_map/mij,mjk->mik/dot_general | solution.py:23
  92.7 2.1 %fusion.13 = f32[4,64,64]{2,1,0:T(8,128)S(1)} fusion(f32[4,64,2048]{2,1,0:T(8,128)S(1)} %convolution_add_fusion.1), kind=kOutput, calls=%fused_computation.27 | convolution fusion | flops 402653184 | bytes 2162688 | tf_op jit(solution)/shard_map/mik,mjk->mij/dot_general | solution.py:19
  94.8 0.3 fusion.3
  95.0 2.1 %convolution_add_fusion = f32[4,64,2048]{2,1,0:T(8,128)S(1)} fusion(f32[4,64,64]{2,1,0:T(8,128)S(1)} %fusion.3, f32[4,64,2048]{2,1,0:T(8,128)S(1)} %convolution_add_fusion.1), kind=kOutput, calls=%fused_computation | convolution fusion | flops 403701760 | bytes 4259840 | tf_op jit(solution)/shard_map/mij,mjk->mik/dot_general | solution.py:23
  97.1 3.2 %copy.33 = f32[4,64,2048]{1,0,2:T(4,128)} copy(f32[4,64,2048]{2,1,0:T(8,128)S(1)} %convolution_add_fusion) | data formatting | bytes 4194304 | tf_op jit(solution)/shard_map/add | solution.py:23
  100.3 6.8 %reshape.10 = f32[8,1,65536]{2,1,0:T(1,128)S(1)} reshape(f32[2048,4,64]{2,1,0:T(4,128)} %bitcast.52) | data formatting | bytes 4194304
  107.1 30.7 %all_to_all.74 = f32[8,1,65536]{2,1,0:T(1,128)} all-to-all(f32[8,1,65536]{2,1,0:T(1,128)S(1)} %reshape.10), channel_id=1, replica_groups=mesh['rows'=16,'cols'=8] {'cols'}, dimensions={0} | all-to-all | bytes 4194304 | tf_op jit(solution)/shard_map/all_to_all | solution.py:26
  137.8 0.5 broadcast.37
  138.3 7.2 %reduce.1 = f32[8,65536]{1,0:T(8,128)S(1)} reduce(f32[8,1,65536]{2,1,0:T(1,128)} %all_to_all.74, f32[]{:T(128)} %broadcast.37), dimensions={1}, to_apply=%all_to_all.60.reduce_sub_computation | reduce | bytes 4194308 | tf_op jit(solution)/shard_map/all_to_all | solution.py:26
  145.5 4.8 %reshape.11 = f32[2048,4,64]{2,1,0:T(4,128)} reshape(f32[8,65536]{1,0:T(8,128)S(1)} %reduce.1) | data formatting | bytes 4194304
  150.3 3.5 %copy.41 = f32[4,64,8,256]{3,1,0,2:T(8,128)S(1)} copy(f32[4,64,8,256]{1,0,3,2:T(4,128)} %bitcast.53) | data formatting | bytes 4194304 | tf_op jit(solution)/shard_map/all_to_all | solution.py:26
  153.8 1.2 copy.36
  155.1 31.6 %all_to_all.75 = f32[32,64,256]{2,0,1:T(8,128)S(1)} all-to-all(f32[32,64,256]{2,0,1:T(8,128)S(1)} %copy.36), channel_id=1, replica_groups=mesh['rows'=16,'cols'=8] {'rows'}, dimensions={1} | all-to-all | bytes 4194304 | tf_op jit(solution)/shard_map/all_to_all | solution.py:27
  186.6 0.0 copy-start.1
  186.6 0.2 copy.37
  186.9 1.3 copy-done.1
  188.2 0.4 bitcast_subtract_fusion
  188.7 2.7 %copy.39 = f32[512,4,256]{2,1,0:T(4,128)} copy(f32[512,4,256]{2,0,1:T(8,128)S(1)} %bitcast_subtract_fusion) | data formatting | bytes 4194304
  (1 shorter events, 0.0 us)
Async XLA Ops:
  3.6 37.0 %copy-start = (f32[512,4,256]{2,1,0:T(4,128)}, f32[512,4,256]{2,1,0:T(4,128)S(1)}, u32[]{:S(2)}) copy-start(f32[512,4,256]{2,1,0:T(4,128)S(1)} %multiply_add_fusion) | copy-start | bytes 6291460
  186.6 1.6 copy-start.1
where the time goes:
time: 195 us; the launch traced here: 192 us
  blocking collectives  131 us (67%)
  local copies, waits for them, and re-layouts  26.4 us (14%)
  matrix products  22.6 us (12%)
  other arithmetic  10.9 us (6%)
    all_to_all x1, blocking collectives, on_device(): lax.all_to_all(new_momentum, 'rows', split_axis=0, concat_axis=1, tiled=T...  37 us
    all_to_all x1, blocking collectives, on_device(): lax.all_to_all(iterate, 'rows', split_axis=1, concat_axis=0, tiled=True)  31.6 us
    all_to_all x1, blocking collectives, on_device(): lax.all_to_all(moved, 'cols', split_axis=0, concat_axis=2, tiled=True)  31.4 us
    all_to_all x1, blocking collectives, on_device(): lax.all_to_all(iterate, 'cols', split_axis=2, concat_axis=0, tiled=True)  30.7 us
    unnamed x7, local copies, waits for them, and re-layouts  15.6 us
    dot_general x5, matrix products, on_device(): jnp.einsum('mij,mjk->mik', mixed, iterate, precision=lax.Precision.HIGHEST)  10.7 us
    dot_general x5, matrix products, on_device(): jnp.einsum('mik,mjk->mij', iterate, iterate, precision=lax.Precision.HIGH...  10.6 us
    all_to_all x1, other arithmetic, on_device(): lax.all_to_all(iterate, 'cols', split_axis=2, concat_axis=0, tiled=True)  7.22 us

commit v1 on v0

v1 whole, which is shorter than its diff:
```python
import functools
import itertools

import jax
import jax.numpy as jnp
from jax import lax
from jax.experimental import pallas as pl
from jax.experimental.pallas import tpu as pltpu
from jax.sharding import PartitionSpec as P

hold_rate = 0.95
learn_rate = 1.0
LINEAR, CUBIC, QUINTIC = 3.4445, -4.775, 2.0315

MESH = pl.DeviceIdType.MESH
STAGES = 2
HIGHEST = lax.Precision.HIGHEST


def send_order():
    def put(axes, values):
        offset = [0, 0, 0]
        for axis, value in zip(axes, values):
            offset[axis] = value % 4
        return tuple(offset)

    rounds = [[(2, 2, 2)]]
    for a, b in itertools.product((1, -1), repeat=2):
        rounds.append([put((0, 1, 2), (1, a, b)), put((0, 1, 2), (-1, -a, -b))])
    for d in range(3):
        e, f = [axis for axis in range(3) if axis != d]
        for a, b in itertools.product((1, -1), repeat=2):
            rounds.append([put((d, e, f), (2, a, b)), put((d, e, f), (0, -a, -b))])
        for a in (1, -1):
            rounds.append([put((d, e, f), (a, 2, 2)), put((d, e, f), (-a, 0, 0))])
        rounds.append([put((d, e, f), (0, 2, 2)), put((d, e, f), (2, 0, 0))])
        for a in (1, -1):
            rounds.append([put((d, e, f), (a, 2, 0)), put((d, e, f), (-a, 0, 2))])
    order = [(0, 0, 0, 1)]
    for group in rounds:
        for core in range(2):
            order += [offset + (core,) for offset in group]
    assert len(set(order)) == 127
    return order


ORDER = send_order()


def mixing(gram, eye, steps):
    mix = None
    for step in range(steps):
        square = jnp.dot(gram, gram, precision=HIGHEST)
        poly = LINEAR * eye + CUBIC * gram + QUINTIC * square
        mix = poly if mix is None else jnp.dot(poly, mix, precision=HIGHEST)
        if step < steps - 1:
            gram = jnp.dot(poly, jnp.dot(gram, poly, precision=HIGHEST), precision=HIGHEST)
    return mix


def kernel(x_ref, out_ref, taken, made, sent, got, back_sent, back_got):
    row, col = lax.axis_index("rows"), lax.axis_index("cols")
    z, y, x, core = row // 4, row % 4, col // 2, col % 2
    zs = [lax.rem(z + d, 4) for d in range(4)]
    ys = [lax.rem(y + d, 4) for d in range(4)]
    xs = [lax.rem(x + d, 4) for d in range(4)]
    cores = [core, 1 - core]
    rows = {(a, b): zs[a] * 4 + ys[b] for a in range(4) for b in range(4)}
    cols = {(a, b): xs[a] * 2 + cores[b] for a in range(4) for b in range(2)}
    places = [(rows[dz, dy], cols[dx, dc]) for dz, dy, dx, dc in ORDER]
    each = 4 // STAGES
    me = row * 8 + col

    barrier = pltpu.get_barrier_semaphore()
    for place in places:
        pl.semaphore_signal(barrier, inc=1, device_id=place, device_id_type=MESH)
    pl.semaphore_wait(barrier, len(places))

    for stage in range(STAGES):
        pltpu.make_async_copy(
            x_ref.at[pl.ds(me * 4 + stage * each, each)], taken.at[stage, row, col], got.at[stage]
        ).start()
        for place in places:
            pltpu.make_async_remote_copy(
                src_ref=x_ref.at[pl.ds((place[0] * 8 + place[1]) * 4 + stage * each, each)],
                dst_ref=taken.at[stage, row, col],
                send_sem=sent.at[stage],
                recv_sem=got.at[stage],
                device_id=place,
                device_id_type=MESH,
            ).start()

    up = lax.broadcasted_iota(jnp.int32, (128, 128), 0)
    across = lax.broadcasted_iota(jnp.int32, (128, 128), 1)
    same_half = (up // 4) % 2 == (across // 4) % 2
    upper = (across // 4) % 2 == 1
    eye = jnp.where(up == across, 1.0, 0.0).astype(jnp.float32)

    def gram_of(blocks):
        wide = jnp.concatenate(blocks, axis=1)
        both = lax.dot_general(wide, wide, (((1,), (1,)), ((), ())), precision=HIGHEST)
        both = jnp.where(same_half, both, 0.0)
        other = pltpu.roll(both.reshape(16, 8, 128), 4, 1).reshape(128, 128)
        other = jnp.where(upper, pltpu.roll(other, 4, 1), pltpu.roll(other, 124, 1))
        return both + other

    for stage in range(STAGES):
        pltpu.make_async_copy(taken.at[stage], taken.at[stage], got.at[stage]).wait()
        for mat in range(each):
            blocks = [taken[stage, :, c, mat].reshape(128, 128) for c in range(8)]
            gram = gram_of(blocks)
            total = 0.5 * jnp.sum(jnp.where(up == across, gram, 0.0), keepdims=True)
            scale = lax.rsqrt(total + 1e-06)
            mix = mixing(gram * (scale * scale), eye, 2) * scale
            blocks = [jnp.dot(mix, block, precision=HIGHEST) for block in blocks]
            mix = mixing(gram_of(blocks), eye, 3)
            for c in range(8):
                made[stage, :, c, mat] = jnp.dot(mix, blocks[c], precision=HIGHEST).reshape(16, 8, 128)
        pltpu.make_async_copy(
            made.at[stage, row, col], out_ref.at[pl.ds(me * 4 + stage * each, each)], back_got.at[stage]
        ).start()
        for place in places:
            pltpu.make_async_remote_copy(
                src_ref=made.at[stage, place[0], place[1]],
                dst_ref=out_ref.at[pl.ds(me * 4 + stage * each, each)],
                send_sem=back_sent.at[stage],
                recv_sem=back_got.at[stage],
                device_id=place,
                device_id_type=MESH,
            ).start()

    whole = out_ref.at[pl.ds(0, 128 * each)]
    part = out_ref.at[pl.ds(0, 127 * each)]
    for stage in range(STAGES):
        pltpu.make_async_copy(whole, whole, back_got.at[stage]).wait()
    for stage in range(STAGES):
        pltpu.make_async_copy(part, part, sent.at[stage]).wait()
        pltpu.make_async_copy(part, part, back_sent.at[stage]).wait()


def on_device(grad_stack, moment_stack, weight_stack):
    mats = grad_stack.shape[0]
    new_momentum = hold_rate * moment_stack + grad_stack
    tiles = new_momentum.reshape(mats, 4, 2, 128).transpose(0, 2, 1, 3).reshape(mats, 8, 128)
    each = 4 // STAGES
    back = pl.pallas_call(
        kernel,
        out_shape=jax.ShapeDtypeStruct((mats, 8, 128), jnp.float32),
        in_specs=[pl.BlockSpec(memory_space=pltpu.VMEM)],
        out_specs=pl.BlockSpec(memory_space=pltpu.VMEM),
        scratch_shapes=[
            pltpu.VMEM((STAGES, 16, 8, each, 8, 128), jnp.float32),
            pltpu.VMEM((STAGES, 16, 8, each, 8, 128), jnp.float32),
            pltpu.SemaphoreType.DMA((STAGES,)),
            pltpu.SemaphoreType.DMA((STAGES,)),
            pltpu.SemaphoreType.DMA((STAGES,)),
            pltpu.SemaphoreType.DMA((STAGES,)),
        ],
        compiler_params=pltpu.CompilerParams(
            collective_id=1, has_side_effects=True, vmem_limit_bytes=48 * 1024 * 1024
        ),
    )(tiles)
    back = back.reshape(mats, 2, 4, 128).transpose(0, 2, 1, 3).reshape(mats, 4, 256)
    new_weights = weight_stack - learn_rate * back
    return (new_weights, new_momentum)


def solution(mesh):
    placed = (P(None, "rows", "cols"), P(None, "rows", "cols"), P(None, "rows", "cols"))
    return jax.shard_map(
        on_device,
        mesh=mesh,
        in_specs=placed,
        out_specs=(P(None, "rows", "cols"), P(None, "rows", "cols")),
        check_vma=False,
    )
```

time: 195 us -> 80.6 us (0.41)
  the two profiles are of different devices: /device:TPU:0 before, /device:TPU:1 now
where the time goes in v1:
time: 80.6 us; the launch traced here: 79.8 us
  Pallas kernels  74.3 us (92%)
  other arithmetic  4.8 us (6%)
    pallas_call x1, Pallas kernels, on_device(): pl.pallas_call(kernel, out_shape=jax.ShapeDtypeStruct((mats, 8, 128), jnp...  74.3 us
    add x1, other arithmetic, on_device(): new_momentum = hold_rate * moment_stack + grad_stack  2.94 us
    sub x1, other arithmetic, on_device(): new_weights = weight_stack - learn_rate * back  1.86 us

profile of v1, /device:TPU:1, one launch (start us, length us, event | category | flops | bytes accessed | tf_op | source)
XLA Modules:
  0.0 79.8 jit_solution(10049528869051665710)
XLA Ops:
  0.6 2.9 %multiply_add_fusion = f32[512,4,256]{2,1,0:T(4,128)S(1)} fusion(f32[512,4,256]{2,1,0:T(4,128)} %param.3, f32[512,4,256]{2,1,0:T(4,128)} %param.4), kind=kLoop, calls=%fused_computation | loop fusion | flops 1048576 | bytes 6291456 | tf_op jit(solution)/shard_map/add | solution.py:143
  3.6 0.0 copy-start
  3.6 0.0 copy-start.1
  3.6 74.3 %shard_map.50 = f32[512,8,128]{2,1,0:T(8,128)S(1)} custom-call(f32[512,8,128]{2,1,0:T(8,128)S(1)} %bitcast.10), custom_call_target="tpu_custom_call" | custom-call | tf_op jit(solution)/shard_map/pallas_call | solution.py:146
  77.9 0.0 copy-done
  77.9 0.0 copy-done.1
  77.9 1.9 %sub.3 = f32[512,4,256]{2,1,0:T(4,128)} subtract(f32[512,4,256]{2,1,0:T(4,128)S(1)} %copy-done.1, f32[512,4,256]{2,1,0:T(4,128)S(1)} %bitcast.11) | non-fusion elementwise | flops 524288 | bytes 6291456 | tf_op jit(solution)/shard_map/sub | solution.py:164
Async XLA Ops:
  3.6 74.3 %copy-start = (f32[512,4,256]{2,1,0:T(4,128)}, f32[512,4,256]{2,1,0:T(4,128)S(1)}, u32[]{:S(2)}) copy-start(f32[512,4,256]{2,1,0:T(4,128)S(1)} %multiply_add_fusion) | copy-start | bytes 6291460
  3.6 74.3 %copy-start.1 = (f32[512,4,256]{2,1,0:T(4,128)S(1)}, f32[512,4,256]{2,1,0:T(4,128)}, u32[]{:S(2)}) copy-start(f32[512,4,256]{2,1,0:T(4,128)} %param.5) | copy-start | bytes 6291460

commit v2 on v1

--- a/solution.py
+++ b/solution.py
@@ -13,7 +13,7 @@
 LINEAR, CUBIC, QUINTIC = 3.4445, -4.775, 2.0315
 
 MESH = pl.DeviceIdType.MESH
-STAGES = 2
+STAGES = 4
 HIGHEST = lax.Precision.HIGHEST
 
 

time: 80.6 us -> 67.5 us (0.84)
  Pallas kernels: 74.3 us -> 61.9 us
    pallas_call x1, Pallas kernels: 74.3 us -> 61.9 us  [on_device(): pl.pallas_call(kernel, out_shape=jax.ShapeDtypeStruct((mats, 8, 128), jnp...]
where the time goes in v2:
time: 67.5 us; the launch traced here: 67.4 us
  Pallas kernels  61.9 us (92%)
  other arithmetic  4.8 us (7%)
    pallas_call x1, Pallas kernels, on_device(): pl.pallas_call(kernel, out_shape=jax.ShapeDtypeStruct((mats, 8, 128), jnp...  61.9 us
    add x1, other arithmetic, on_device(): new_momentum = hold_rate * moment_stack + grad_stack  2.94 us
    sub x1, other arithmetic, on_device(): new_weights = weight_stack - learn_rate * back  1.86 us

profile of v2, /device:TPU:1, one launch (start us, length us, event | category | flops | bytes accessed | tf_op | source)
XLA Modules:
  0.0 67.4 jit_solution(15859552044621350969)
XLA Ops:
  0.6 2.9 %multiply_add_fusion = f32[512,4,256]{2,1,0:T(4,128)S(1)} fusion(f32[512,4,256]{2,1,0:T(4,128)} %param.3, f32[512,4,256]{2,1,0:T(4,128)} %param.4), kind=kLoop, calls=%fused_computation | loop fusion | flops 1048576 | bytes 6291456 | tf_op jit(solution)/shard_map/add | solution.py:143
  3.6 0.0 copy-start
  3.6 0.0 copy-start.1
  3.6 61.9 %shard_map.50 = f32[512,8,128]{2,1,0:T(8,128)S(1)} custom-call(f32[512,8,128]{2,1,0:T(8,128)S(1)} %bitcast.10), custom_call_target="tpu_custom_call" | custom-call | tf_op jit(solution)/shard_map/pallas_call | solution.py:146
  65.5 0.0 copy-done
  65.5 0.0 copy-done.1
  65.5 1.9 %sub.3 = f32[512,4,256]{2,1,0:T(4,128)} subtract(f32[512,4,256]{2,1,0:T(4,128)S(1)} %copy-done.1, f32[512,4,256]{2,1,0:T(4,128)S(1)} %bitcast.11) | non-fusion elementwise | flops 524288 | bytes 6291456 | tf_op jit(solution)/shard_map/sub | solution.py:164
Async XLA Ops:
  3.6 61.9 %copy-start = (f32[512,4,256]{2,1,0:T(4,128)}, f32[512,4,256]{2,1,0:T(4,128)S(1)}, u32[]{:S(2)}) copy-start(f32[512,4,256]{2,1,0:T(4,128)S(1)} %multiply_add_fusion) | copy-start | bytes 6291460
  3.6 61.9 %copy-start.1 = (f32[512,4,256]{2,1,0:T(4,128)S(1)}, f32[512,4,256]{2,1,0:T(4,128)}, u32[]{:S(2)}) copy-start(f32[512,4,256]{2,1,0:T(4,128)} %param.5) | copy-start | bytes 6291460

commit v3 on v2

--- a/solution.py
+++ b/solution.py
@@ -1,4 +1,3 @@
-import functools
 import itertools
 
 import jax
@@ -14,6 +13,7 @@
 
 MESH = pl.DeviceIdType.MESH
 STAGES = 4
+PIECE = 16
 HIGHEST = lax.Precision.HIGHEST
 
 
@@ -58,7 +58,10 @@
     return mix
 
 
-def kernel(x_ref, out_ref, taken, made, sent, got, back_sent, back_got):
+def kernel(
+    grad_ref, moment_ref, weight_ref, out_ref, x_ref,
+    grad, moment, taken, made, landed, sent, got, back_sent, back_got, loaded, held,
+):
     row, col = lax.axis_index("rows"), lax.axis_index("cols")
     z, y, x, core = row // 4, row % 4, col // 2, col % 2
     zs = [lax.rem(z + d, 4) for d in range(4)]
@@ -68,21 +71,35 @@
     rows = {(a, b): zs[a] * 4 + ys[b] for a in range(4) for b in range(4)}
     cols = {(a, b): xs[a] * 2 + cores[b] for a in range(4) for b in range(2)}
     places = [(rows[dz, dy], cols[dx, dc]) for dz, dy, dx, dc in ORDER]
-    each = 4 // STAGES
     me = row * 8 + col
+
+    pieces = [pl.ds(piece * PIECE, PIECE) for piece in range(128 // PIECE)]
+    loads = []
+    for at, piece in enumerate(pieces):
+        loads.append((
+            pltpu.make_async_copy(grad_ref.at[piece], grad.at[piece], loaded.at[0, at]),
+            pltpu.make_async_copy(moment_ref.at[piece], moment.at[piece], loaded.at[1, at]),
+        ))
+    for pair in loads:
+        for load in pair:
+            load.start()
+    weights = pltpu.make_async_copy(weight_ref, out_ref, held)
+    weights.start()
 
     barrier = pltpu.get_barrier_semaphore()
     for place in places:
         pl.semaphore_signal(barrier, inc=1, device_id=place, device_id_type=MESH)
+    for piece, pair in zip(pieces, loads):
+        for load in pair:
+            load.wait()
+        x_ref[piece] = hold_rate * moment[piece] + grad[piece]
     pl.semaphore_wait(barrier, len(places))
 
     for stage in range(STAGES):
-        pltpu.make_async_copy(
-            x_ref.at[pl.ds(me * 4 + stage * each, each)], taken.at[stage, row, col], got.at[stage]
-        ).start()
+        pltpu.make_async_copy(x_ref.at[me, stage], taken.at[stage, row, col], got.at[stage]).start()
         for place in places:
             pltpu.make_async_remote_copy(
-                src_ref=x_ref.at[pl.ds((place[0] * 8 + place[1]) * 4 + stage * each, each)],
+                src_ref=x_ref.at[place[0] * 8 + place[1], stage],
                 dst_ref=taken.at[stage, row, col],
                 send_sem=sent.at[stage],
                 recv_sem=got.at[stage],
@@ -106,63 +123,90 @@
 
     for stage in range(STAGES):
         pltpu.make_async_copy(taken.at[stage], taken.at[stage], got.at[stage]).wait()
-        for mat in range(each):
-            blocks = [taken[stage, :, c, mat].reshape(128, 128) for c in range(8)]
-            gram = gram_of(blocks)
-            total = 0.5 * jnp.sum(jnp.where(up == across, gram, 0.0), keepdims=True)
-            scale = lax.rsqrt(total + 1e-06)
-            mix = mixing(gram * (scale * scale), eye, 2) * scale
-            blocks = [jnp.dot(mix, block, precision=HIGHEST) for block in blocks]
-            mix = mixing(gram_of(blocks), eye, 3)
-            for c in range(8):
-                made[stage, :, c, mat] = jnp.dot(mix, blocks[c], precision=HIGHEST).reshape(16, 8, 128)
-        pltpu.make_async_copy(
-            made.at[stage, row, col], out_ref.at[pl.ds(me * 4 + stage * each, each)], back_got.at[stage]
-        ).start()
+        blocks = [taken[stage, :, c].reshape(128, 128) for c in range(8)]
+        gram = gram_of(blocks)
+        total = 0.5 * jnp.sum(jnp.where(up == across, gram, 0.0), keepdims=True)
+        scale = lax.rsqrt(total + 1e-06)
+        mix = mixing(gram * (scale * scale), eye, 2) * scale
+        blocks = [jnp.dot(mix, block, precision=HIGHEST) for block in blocks]
+        mix = mixing(gram_of(blocks), eye, 3)
+        for c in range(8):
+            made[stage, :, c] = jnp.dot(mix, blocks[c], precision=HIGHEST).reshape(16, 8, 128)
+        pltpu.make_async_copy(made.at[stage, row, col], landed.at[stage, me], back_got.at[stage]).start()
         for place in places:
             pltpu.make_async_remote_copy(
                 src_ref=made.at[stage, place[0], place[1]],
-                dst_ref=out_ref.at[pl.ds(me * 4 + stage * each, each)],
+                dst_ref=landed.at[stage, me],
                 send_sem=back_sent.at[stage],
                 recv_sem=back_got.at[stage],
                 device_id=place,
                 device_id_type=MESH,
             ).start()
 
-    whole = out_ref.at[pl.ds(0, 128 * each)]
-    part = out_ref.at[pl.ds(0, 127 * each)]
-    for stage in range(STAGES):
-        pltpu.make_async_copy(whole, whole, back_got.at[stage]).wait()
+    weights.wait()
+    for stage in range(STAGES):
+        pltpu.make_async_copy(landed.at[stage], landed.at[stage], back_got.at[stage]).wait()
+        out_ref[:, stage] = out_ref[:, stage] - learn_rate * landed[stage]
+    part = landed.at[0, pl.ds(0, 127)]
     for stage in range(STAGES):
         pltpu.make_async_copy(part, part, sent.at[stage]).wait()
         pltpu.make_async_copy(part, part, back_sent.at[stage]).wait()
 
 
+def write_out(weights, momentum, weights_out, momentum_out, done):
+    copies = [
+        pltpu.make_async_copy(weights, weights_out, done.at[0]),
+        pltpu.make_async_copy(momentum, momentum_out, done.at[1]),
+    ]
+    for copy in copies:
+        copy.start()
+    for copy in copies:
+        copy.wait()
+
+
+def to_tiles(array):
+    return array.reshape(512, 4, 2, 128).transpose(0, 2, 1, 3).reshape(128, 4, 8, 128)
+
+
+def from_tiles(array):
+    return array.reshape(512, 2, 4, 128).transpose(0, 2, 1, 3).reshape(512, 4, 256)
+
+
 def on_device(grad_stack, moment_stack, weight_stack):
-    mats = grad_stack.shape[0]
-    new_momentum = hold_rate * moment_stack + grad_stack
-    tiles = new_momentum.reshape(mats, 4, 2, 128).transpose(0, 2, 1, 3).reshape(mats, 8, 128)
-    each = 4 // STAGES
-    back = pl.pallas_call(
+    tiles = jax.ShapeDtypeStruct((128, 4, 8, 128), jnp.float32)
+    in_vmem = pl.BlockSpec(memory_space=pltpu.VMEM)
+    anywhere = pl.BlockSpec(memory_space=pl.ANY)
+    updated = pl.pallas_call(
         kernel,
-        out_shape=jax.ShapeDtypeStruct((mats, 8, 128), jnp.float32),
-        in_specs=[pl.BlockSpec(memory_space=pltpu.VMEM)],
-        out_specs=pl.BlockSpec(memory_space=pltpu.VMEM),
+        out_shape=(tiles, tiles),
+        in_specs=[anywhere] * 3,
+        out_specs=[in_vmem] * 2,
         scratch_shapes=[
-            pltpu.VMEM((STAGES, 16, 8, each, 8, 128), jnp.float32),
-            pltpu.VMEM((STAGES, 16, 8, each, 8, 128), jnp.float32),
-            pltpu.SemaphoreType.DMA((STAGES,)),
-            pltpu.SemaphoreType.DMA((STAGES,)),
-            pltpu.SemaphoreType.DMA((STAGES,)),
-            pltpu.SemaphoreType.DMA((STAGES,)),
+            pltpu.VMEM((128, 4, 8, 128), jnp.float32),
+            pltpu.VMEM((128, 4, 8, 128), jnp.float32),
+            pltpu.VMEM((STAGES, 16, 8, 8, 128), jnp.float32),
+            pltpu.VMEM((STAGES, 16, 8, 8, 128), jnp.float32),
+            pltpu.VMEM((STAGES, 128, 8, 128), jnp.float32),
+            pltpu.SemaphoreType.DMA((STAGES,)),
+            pltpu.SemaphoreType.DMA((STAGES,)),
+            pltpu.SemaphoreType.DMA((STAGES,)),
+            pltpu.SemaphoreType.DMA((STAGES,)),
+            pltpu.SemaphoreType.DMA((2, 128 // PIECE)),
+            pltpu.SemaphoreType.DMA,
         ],
         compiler_params=pltpu.CompilerParams(
             collective_id=1, has_side_effects=True, vmem_limit_bytes=48 * 1024 * 1024
         ),
-    )(tiles)
-    back = back.reshape(mats, 2, 4, 128).transpose(0, 2, 1, 3).reshape(mats, 4, 256)
-    new_weights = weight_stack - learn_rate * back
-    return (new_weights, new_momentum)
+    )(to_tiles(grad_stack), to_tiles(moment_stack), to_tiles(weight_stack))
+    written = pl.pallas_call(
+        write_out,
+        out_shape=(tiles, tiles),
+        in_specs=[in_vmem] * 2,
+        out_specs=[anywhere] * 2,
+        scratch_shapes=[pltpu.SemaphoreType.DMA((2,))],
+        compiler_params=pltpu.CompilerParams(vmem_limit_bytes=16 * 1024 * 1024),
+    )(*updated)
+    return tuple(from_tiles(array) for array in written)
 
 
 def solution(mesh):

time: 67.5 us -> 64.6 us (0.957)
  other arithmetic: 4.8 us -> 0 us
  Pallas kernels: 61.9 us -> 63.7 us
    add x1 -> x0, other arithmetic: 2.94 us -> none  [on_device(): new_momentum = hold_rate * moment_stack + grad_stack]
    sub x1 -> x0, other arithmetic: 1.86 us -> none  [on_device(): new_weights = weight_stack - learn_rate * back]
    pallas_call x1 -> x2, Pallas kernels: 61.9 us -> 63.7 us  [the longest x1 61.7 us: on_device(): pl.pallas_call(kernel, out_shape=(tiles, tiles), in_specs=[anywhere] * 3,...]
where the time goes in v3:
time: 64.6 us; the launch traced here: 64.5 us
  Pallas kernels  63.7 us (99%)
  between operations  0.8 us (1%)
    pallas_call x1, Pallas kernels, on_device(): pl.pallas_call(kernel, out_shape=(tiles, tiles), in_specs=[anywhere] * 3,...  61.7 us
    pallas_call x1, Pallas kernels, on_device(): pl.pallas_call(write_out, out_shape=(tiles, tiles), in_specs=[in_vmem] *...  2.03 us

profile of v3, /device:TPU:1, one launch (start us, length us, event | category | flops | bytes accessed | tf_op | source)
XLA Modules:
  0.0 64.5 jit_solution(18038670857600682951)
XLA Ops:
  0.6 61.7 %shard_map.50 = (f32[128,4,8,128]{3,2,1,0:T(8,128)S(1)}, f32[128,4,8,128]{3,2,1,0:T(8,128)S(1)}) custom-call(f32[128,4,8,128]{3,2,1,0:T(8,128)} %bitcast.25, f32[128,4,8,128]{3,2,1,0:T(8,128)} %bitcast.26, f32[128,4,8,128]{3,2,1,0:T(8,128)} %bitcast.27), custom_call_target="tpu_custom_call" | custom-call | tf_op jit(solution)/shard_map/pallas_call | solution.py:179
  62.3 2.0 %shard_map.51 = (f32[128,4,8,128]{3,2,1,0:T(8,128)}, f32[128,4,8,128]{3,2,1,0:T(8,128)}) custom-call(f32[128,4,8,128]{3,2,1,0:T(8,128)S(1)} %get-tuple-element.6.weights, f32[128,4,8,128]{3,2,1,0:T(8,128)S(1)} %get-tuple-element.7.momentum), custom_call_target="tpu_custom_call" | custom-call | tf_op jit(solution)/shard_map/pallas_call | solution.py:201

commit v4 on v3

--- a/solution.py
+++ b/solution.py
@@ -14,7 +14,6 @@
 MESH = pl.DeviceIdType.MESH
 STAGES = 4
 PIECE = 16
-HIGHEST = lax.Precision.HIGHEST
 
 
 def send_order():
@@ -47,14 +46,33 @@
 ORDER = send_order()
 
 
+def parts(array):
+    high = array.astype(jnp.bfloat16)
+    rest = array - high.astype(jnp.float32)
+    middle = rest.astype(jnp.bfloat16)
+    return high, middle, (rest - middle.astype(jnp.float32)).astype(jnp.bfloat16)
+
+
+def product(left, right):
+    high, middle, low = left
+    high_right, middle_right, low_right = right
+    side = lambda *arrays: jnp.concatenate(arrays, axis=1)
+    above = lambda *arrays: jnp.concatenate(arrays, axis=0)
+    dot = lambda x, y: jnp.dot(x, y, preferred_element_type=jnp.float32)
+    large = dot(above(side(high, high), side(middle, middle)), above(high_right, middle_right))
+    small = dot(side(low, high), above(high_right, low_right))
+    return large[:128] + (large[128:] + small)
+
+
 def mixing(gram, eye, steps):
     mix = None
     for step in range(steps):
-        square = jnp.dot(gram, gram, precision=HIGHEST)
-        poly = LINEAR * eye + CUBIC * gram + QUINTIC * square
-        mix = poly if mix is None else jnp.dot(poly, mix, precision=HIGHEST)
+        split = parts(gram)
+        poly = LINEAR * eye + CUBIC * gram + QUINTIC * product(split, split)
+        split_poly = parts(poly)
+        mix = poly if mix is None else product(split_poly, parts(mix))
         if step < steps - 1:
-            gram = jnp.dot(poly, jnp.dot(gram, poly, precision=HIGHEST), precision=HIGHEST)
+            gram = product(split_poly, parts(product(split_poly, split)))
     return mix
 
 
@@ -113,9 +131,15 @@
     upper = (across // 4) % 2 == 1
     eye = jnp.where(up == across, 1.0, 0.0).astype(jnp.float32)
 
-    def gram_of(blocks):
-        wide = jnp.concatenate(blocks, axis=1)
-        both = lax.dot_general(wide, wide, (((1,), (1,)), ((), ())), precision=HIGHEST)
+    def gram_of(split):
+        high, middle, low = split
+        both = lax.dot_general(
+            jnp.concatenate(split, axis=0), jnp.concatenate((high, middle), axis=0),
+            (((1,), (1,)), ((), ())), preferred_element_type=jnp.float32,
+        )
+        last = both[256:, :128] + both[256:, 128:]
+        mixed = both[:128, 128:] + both[128:256, :128]
+        both = both[:128, :128] + (mixed + (both[128:256, 128:] + (last + last.T)))
         both = jnp.where(same_half, both, 0.0)
         other = pltpu.roll(both.reshape(16, 8, 128), 4, 1).reshape(128, 128)
         other = jnp.where(upper, pltpu.roll(other, 4, 1), pltpu.roll(other, 124, 1))
@@ -123,15 +147,17 @@
 
     for stage in range(STAGES):
         pltpu.make_async_copy(taken.at[stage], taken.at[stage], got.at[stage]).wait()
-        blocks = [taken[stage, :, c].reshape(128, 128) for c in range(8)]
-        gram = gram_of(blocks)
+        wide = jnp.concatenate([taken[stage, :, c].reshape(128, 128) for c in range(8)], axis=1)
+        split = parts(wide)
+        gram = gram_of(split)
         total = 0.5 * jnp.sum(jnp.where(up == across, gram, 0.0), keepdims=True)
         scale = lax.rsqrt(total + 1e-06)
         mix = mixing(gram * (scale * scale), eye, 2) * scale
-        blocks = [jnp.dot(mix, block, precision=HIGHEST) for block in blocks]
-        mix = mixing(gram_of(blocks), eye, 3)
+        split = parts(product(parts(mix), split))
+        mix = mixing(gram_of(split), eye, 3)
+        wide = product(parts(mix), split)
         for c in range(8):
-            made[stage, :, c] = jnp.dot(mix, blocks[c], precision=HIGHEST).reshape(16, 8, 128)
+            made[stage, :, c] = wide[:, c * 128 : c * 128 + 128].reshape(16, 8, 128)
         pltpu.make_async_copy(made.at[stage, row, col], landed.at[stage, me], back_got.at[stage]).start()
         for place in places:
             pltpu.make_async_remote_copy(

time: 64.6 us -> 67.4 us (1.043)
  Pallas kernels: 63.7 us -> 66.5 us
    pallas_call x1, Pallas kernels: 61.7 us -> 64.4 us  [on_device(): pl.pallas_call(kernel, out_shape=(tiles, tiles), in_specs=[anywhere] * 3,...]
where the time goes in v4:
time: 67.4 us; the launch traced here: 67.3 us
  Pallas kernels  66.5 us (99%)
  between operations  0.8 us (1%)
    pallas_call x1, Pallas kernels, on_device(): pl.pallas_call(kernel, out_shape=(tiles, tiles), in_specs=[anywhere] * 3,...  64.4 us
    pallas_call x1, Pallas kernels, on_device(): pl.pallas_call(write_out, out_shape=(tiles, tiles), in_specs=[in_vmem] *...  2.03 us

profile of v4, /device:TPU:1, one launch (start us, length us, event | category | flops | bytes accessed | tf_op | source)
XLA Modules:
  0.0 67.3 jit_solution(10733702665340434425)
XLA Ops:
  0.6 64.4 %shard_map.50 = (f32[128,4,8,128]{3,2,1,0:T(8,128)S(1)}, f32[128,4,8,128]{3,2,1,0:T(8,128)S(1)}) custom-call(f32[128,4,8,128]{3,2,1,0:T(8,128)} %bitcast.25, f32[128,4,8,128]{3,2,1,0:T(8,128)} %bitcast.26, f32[128,4,8,128]{3,2,1,0:T(8,128)} %bitcast.27), custom_call_target="tpu_custom_call" | custom-call | tf_op jit(solution)/shard_map/pallas_call | solution.py:205
  65.1 2.0 %shard_map.51 = (f32[128,4,8,128]{3,2,1,0:T(8,128)}, f32[128,4,8,128]{3,2,1,0:T(8,128)}) custom-call(f32[128,4,8,128]{3,2,1,0:T(8,128)S(1)} %get-tuple-element.6.weights, f32[128,4,8,128]{3,2,1,0:T(8,128)S(1)} %get-tuple-element.7.momentum), custom_call_target="tpu_custom_call" | custom-call | tf_op jit(solution)/shard_map/pallas_call | solution.py:227

commit v5 on v4

--- a/solution.py
+++ b/solution.py
@@ -16,34 +16,24 @@
 PIECE = 16
 
 
-def send_order():
-    def put(axes, values):
-        offset = [0, 0, 0]
-        for axis, value in zip(axes, values):
-            offset[axis] = value % 4
-        return tuple(offset)
-
-    rounds = [[(2, 2, 2)]]
-    for a, b in itertools.product((1, -1), repeat=2):
-        rounds.append([put((0, 1, 2), (1, a, b)), put((0, 1, 2), (-1, -a, -b))])
-    for d in range(3):
-        e, f = [axis for axis in range(3) if axis != d]
-        for a, b in itertools.product((1, -1), repeat=2):
-            rounds.append([put((d, e, f), (2, a, b)), put((d, e, f), (0, -a, -b))])
-        for a in (1, -1):
-            rounds.append([put((d, e, f), (a, 2, 2)), put((d, e, f), (-a, 0, 0))])
-        rounds.append([put((d, e, f), (0, 2, 2)), put((d, e, f), (2, 0, 0))])
-        for a in (1, -1):
-            rounds.append([put((d, e, f), (a, 2, 0)), put((d, e, f), (-a, 0, 2))])
-    order = [(0, 0, 0, 1)]
-    for group in rounds:
-        for core in range(2):
-            order += [offset + (core,) for offset in group]
-    assert len(set(order)) == 127
-    return order
-
-
-ORDER = send_order()
+def by_distance():
+    levels = {}
+    for core in range(2):
+        for offset in itertools.product(range(4), repeat=3):
+            if any(offset) or core:
+                hops = max(1, sum(min(d, 4 - d) for d in offset))
+                levels.setdefault(hops, []).append(offset + (core,))
+
+    def twins(offset):
+        opposite = tuple(-d % 4 for d in offset[:3])
+        turn = sum(1 for d in offset[:3] if d == 2)
+        return (turn, max(offset[:3], opposite), offset[3], offset)
+
+    return [sorted(levels[hops], key=twins) for hops in sorted(levels)]
+
+
+LEVELS = by_distance()
+NEAR = 2
 
 
 def parts(array):
@@ -78,7 +68,7 @@
 
 def kernel(
     grad_ref, moment_ref, weight_ref, out_ref, x_ref,
-    grad, moment, taken, made, landed, sent, got, back_sent, back_got, loaded, held,
+    grad, moment, taken, made, landed, sent, got, back_sent, back_got, loaded, held, near,
 ):
     row, col = lax.axis_index("rows"), lax.axis_index("cols")
     z, y, x, core = row // 4, row % 4, col // 2, col % 2
@@ -88,7 +78,7 @@
     cores = [core, 1 - core]
     rows = {(a, b): zs[a] * 4 + ys[b] for a in range(4) for b in range(4)}
     cols = {(a, b): xs[a] * 2 + cores[b] for a in range(4) for b in range(2)}
-    places = [(rows[dz, dy], cols[dx, dc]) for dz, dy, dx, dc in ORDER]
+    levels = [[(rows[dz, dy], cols[dx, dc]) for dz, dy, dx, dc in level] for level in LEVELS]
     me = row * 8 + col
 
     pieces = [pl.ds(piece * PIECE, PIECE) for piece in range(128 // PIECE)]
@@ -104,18 +94,15 @@
     weights = pltpu.make_async_copy(weight_ref, out_ref, held)
     weights.start()
 
-    barrier = pltpu.get_barrier_semaphore()
-    for place in places:
-        pl.semaphore_signal(barrier, inc=1, device_id=place, device_id_type=MESH)
-    for piece, pair in zip(pieces, loads):
-        for load in pair:
-            load.wait()
-        x_ref[piece] = hold_rate * moment[piece] + grad[piece]
-    pl.semaphore_wait(barrier, len(places))
-
-    for stage in range(STAGES):
-        pltpu.make_async_copy(x_ref.at[me, stage], taken.at[stage, row, col], got.at[stage]).start()
-        for place in places:
+    def tell(semaphore):
+        for place in levels[0]:
+            pl.semaphore_signal(semaphore, inc=1, device_id=place, device_id_type=MESH)
+
+    def hear(semaphore):
+        pl.semaphore_wait(semaphore, len(levels[0]))
+
+    def send(stage, level):
+        for place in level:
             pltpu.make_async_remote_copy(
                 src_ref=x_ref.at[place[0] * 8 + place[1], stage],
                 dst_ref=taken.at[stage, row, col],
@@ -124,6 +111,29 @@
                 device_id=place,
                 device_id_type=MESH,
             ).start()
+
+    tell(pltpu.get_barrier_semaphore())
+    hear(pltpu.get_barrier_semaphore())
+    tell(near.at[0])
+    for piece, pair in zip(pieces, loads):
+        for load in pair:
+            load.wait()
+        x_ref[piece] = hold_rate * moment[piece] + grad[piece]
+    hear(near.at[0])
+    tell(near.at[1])
+    for stage in range(STAGES):
+        pltpu.make_async_copy(x_ref.at[me, stage], taken.at[stage, row, col], got.at[stage]).start()
+    for level in levels[:NEAR]:
+        for stage in range(STAGES):
+            send(stage, level)
+    for hops in range(NEAR, len(levels)):
+        hear(near.at[hops - 1])
+        if hops < len(levels) - 1:
+            tell(near.at[hops])
+        send(0, levels[hops])
+    for stage in range(1, STAGES):
+        for level in levels[NEAR:]:
+            send(stage, level)
 
     up = lax.broadcasted_iota(jnp.int32, (128, 128), 0)
     across = lax.broadcasted_iota(jnp.int32, (128, 128), 1)
@@ -159,7 +169,7 @@
         for c in range(8):
             made[stage, :, c] = wide[:, c * 128 : c * 128 + 128].reshape(16, 8, 128)
         pltpu.make_async_copy(made.at[stage, row, col], landed.at[stage, me], back_got.at[stage]).start()
-        for place in places:
+        for place in itertools.chain(*reversed(levels)):
             pltpu.make_async_remote_copy(
                 src_ref=made.at[stage, place[0], place[1]],
                 dst_ref=landed.at[stage, me],
@@ -219,6 +229,7 @@
             pltpu.SemaphoreType.DMA((STAGES,)),
             pltpu.SemaphoreType.DMA((2, 128 // PIECE)),
             pltpu.SemaphoreType.DMA,
+            pltpu.SemaphoreType.REGULAR((len(LEVELS) - 1,)),
         ],
         compiler_params=pltpu.CompilerParams(
             collective_id=1, has_side_effects=True, vmem_limit_bytes=48 * 1024 * 1024

time: 67.4 us -> 68.9 us (1.022)
  Pallas kernels: 66.5 us -> 68 us
    pallas_call x1, Pallas kernels: 64.4 us -> 66 us  [on_device(): pl.pallas_call(kernel, out_shape=(tiles, tiles), in_specs=[anywhere] * 3,...]
where the time goes in v5:
time: 68.9 us; the launch traced here: 68.8 us
  Pallas kernels  68 us (99%)
  between operations  0.8 us (1%)
    pallas_call x1, Pallas kernels, on_device(): pl.pallas_call(kernel, out_shape=(tiles, tiles), in_specs=[anywhere] * 3,...  66 us
    pallas_call x1, Pallas kernels, on_device(): pl.pallas_call(write_out, out_shape=(tiles, tiles), in_specs=[in_vmem] *...  2.03 us

profile of v5, /device:TPU:1, one launch (start us, length us, event | category | flops | bytes accessed | tf_op | source)
XLA Modules:
  0.0 68.8 jit_solution(11294177816349752896)
XLA Ops:
  0.6 66.0 %shard_map.50 = (f32[128,4,8,128]{3,2,1,0:T(8,128)S(1)}, f32[128,4,8,128]{3,2,1,0:T(8,128)S(1)}) custom-call(f32[128,4,8,128]{3,2,1,0:T(8,128)} %bitcast.25, f32[128,4,8,128]{3,2,1,0:T(8,128)} %bitcast.26, f32[128,4,8,128]{3,2,1,0:T(8,128)} %bitcast.27), custom_call_target="tpu_custom_call" | custom-call | tf_op jit(solution)/shard_map/pallas_call | solution.py:215
  66.6 2.0 %shard_map.51 = (f32[128,4,8,128]{3,2,1,0:T(8,128)}, f32[128,4,8,128]{3,2,1,0:T(8,128)}) custom-call(f32[128,4,8,128]{3,2,1,0:T(8,128)S(1)} %get-tuple-element.6.weights, f32[128,4,8,128]{3,2,1,0:T(8,128)S(1)} %get-tuple-element.7.momentum), custom_call_target="tpu_custom_call" | custom-call | tf_op jit(solution)/shard_map/pallas_call | solution.py:238
